TPU v7x, 512 devices: a whole 4x8x8 slice. The times are simulated.
512 devices in a mesh: expert: 128 (over x, z, y_lo), hidden: 4 (over y_hi, core).
Axes of the slice: x: 4, y: 8 (y_hi: 2, y_lo: 4; y = y_hi * 4 + y_lo), z: 8, core: 2. Of those that a mesh axis runs over, the one named last changes fastest.
Arguments:
- tokens: bfloat16 [512, 196, 1024], P(('expert', 'hidden')), may hold values from -40 to 40
- router: bfloat16 [1024, 128], replicated, may hold values from -0.5 to 0.5
- w_in: bfloat16 [128, 1024, 3072], P('expert', None, 'hidden'), may hold values from -0.1875 to 0.1875
- b_in: float32 [128, 3072], P('expert', 'hidden'), may hold values from -6 to 6
- w_out: bfloat16 [128, 3072, 1024], P('expert', 'hidden'), may hold values from -0.109375 to 0.109375
- cotangent: bfloat16 [512, 196, 1024], P(('expert', 'hidden')), may hold values from -6 to 6
Outputs:
- mixed: bfloat16 [512, 196, 1024], P(('expert', 'hidden'))
- token_grad: bfloat16 [512, 196, 1024], P(('expert', 'hidden'))
All inputs are finite; a program needn't handle non-finite values.
Results may differ from a plain program's by a relative error of at most 0.015.
Values may be sent and summed in bfloat16 or wider, within the bound.
No kernel may reach another device: no remote copies, remote signals or barrier semaphores. Data moves between devices by JAX's collectives and lax.ppermute only.
A program may use at most 64 MiB of HBM per device.

v0:
```python
import jax
import jax.numpy as jnp
from jax import lax
from jax.sharding import PartitionSpec as P


def split_up(x, dim, devices):
    shape = x.shape
    parts = x.reshape(*shape[:dim], devices, shape[dim] // devices, *shape[dim + 1 :])
    return jnp.moveaxis(parts, dim, 0)


def sum_at_owner(x, axis, dim):
    devices = lax.axis_size(axis)
    parts = lax.all_to_all(split_up(x, dim, devices), axis, 0, 0, tiled=True)
    return jnp.sum(parts.astype(jnp.float32), axis=0)


def outbound(stacked):
    moved = lax.all_to_all(stacked, "expert", split_axis=2, concat_axis=1, tiled=True)
    return lax.all_gather(moved, "hidden", axis=1, tiled=True)


def inbound(terms):
    summed = sum_at_owner(terms.astype(jnp.bfloat16), "hidden", 1)
    return lax.all_to_all(
        summed.astype(jnp.bfloat16), "expert", split_axis=1, concat_axis=2, tiled=True
    )


def expert_forward(slots, w_in, b_in, w_out):
    pre = jnp.einsum("red,edf->ref", slots, w_in, preferred_element_type=jnp.float32) + b_in[None]
    act = jax.nn.gelu(pre).astype(jnp.bfloat16)
    return (jnp.einsum("ref,efd->red", act, w_out, preferred_element_type=jnp.float32), pre)


def expert_backward(grads, pre, w_in, w_out):
    act_grad = jnp.einsum("red,efd->ref", grads, w_out, preferred_element_type=jnp.float32)
    _, pull = jax.vjp(jax.nn.gelu, pre)
    pre_grad = pull(act_grad)[0].astype(jnp.bfloat16)
    return jnp.einsum("ref,edf->red", pre_grad, w_in, preferred_element_type=jnp.float32)


def shards(tokens, router, w_in, b_in, w_out, cotangent):
    logits = jnp.einsum("bmd,ds->bms", tokens, router, preferred_element_type=jnp.float32)
    dispatch = jax.nn.softmax(logits, axis=1)
    combine = jax.nn.softmax(logits, axis=2)
    dispatch_w = dispatch.astype(jnp.bfloat16)
    combine_w = combine.astype(jnp.bfloat16)
    slot_in = jnp.einsum(
        "bms,bmd->bsd", dispatch_w, tokens, preferred_element_type=jnp.float32
    ).astype(jnp.bfloat16)
    slot_cot = jnp.einsum(
        "bms,bmd->bsd", combine_w, cotangent, preferred_element_type=jnp.float32
    ).astype(jnp.bfloat16)
    arrived = outbound(jnp.stack([slot_in, slot_cot]))
    partial_value, pre = expert_forward(arrived[0], w_in, b_in, w_out)
    gpartial = expert_backward(arrived[1], pre, w_in, w_out)
    returned = inbound(jnp.stack([partial_value, gpartial]))
    slot_out = returned[0]
    slot_grad = returned[1]
    mixed = jnp.einsum(
        "bms,bsd->bmd", combine_w, slot_out, preferred_element_type=jnp.float32
    ).astype(jnp.bfloat16)
    combine_grad = jnp.einsum(
        "bmd,bsd->bms", cotangent, slot_out, preferred_element_type=jnp.float32
    )
    dispatch_grad = jnp.einsum(
        "bmd,bsd->bms", tokens, slot_grad, preferred_element_type=jnp.float32
    )
    logit_grad = combine * (combine_grad - jnp.sum(combine * combine_grad, axis=2, keepdims=True))
    logit_grad = logit_grad + dispatch * (
        dispatch_grad - jnp.sum(dispatch * dispatch_grad, axis=1, keepdims=True)
    )
    logit_grad = logit_grad.astype(jnp.bfloat16)
    token_grad = jnp.einsum(
        "bms,bsd->bmd", dispatch_w, slot_grad, preferred_element_type=jnp.float32
    )
    token_grad = token_grad + jnp.einsum(
        "bms,ds->bmd", logit_grad, router, preferred_element_type=jnp.float32
    )
    return (mixed, token_grad.astype(jnp.bfloat16))


def solution(mesh):
    return jax.shard_map(
        shards,
        mesh=mesh,
        in_specs=(
            P(("expert", "hidden"), None, None),
            P(),
            P("expert", None, "hidden"),
            P("expert", "hidden"),
            P("expert", "hidden", None),
            P(("expert", "hidden"), None, None),
        ),
        out_specs=(P(("expert", "hidden"), None, None), P(("expert", "hidden"), None, None)),
        check_vma=False,
    )
```

profile of v0, /device:TPU:1, one launch (start us, length us, event | category | flops | bytes accessed | tf_op | source)
XLA Modules:
  0.0 200.0 jit_solution(14822342059811094486)
XLA Ops:
  7.2 0.0 copy-start
  7.2 0.0 all-gather.3.cloned.1.call-start
  7.2 1.6 fusion.82
  8.8 0.2 fusion.59
  9.0 1.3 fusion.35
  10.3 0.0 copy-done.3
  10.3 0.4 fusion.36
  10.7 0.1 pad_maximum_fusion
  10.7 0.5 copy.17
  11.3 0.0 copy-start.4
  11.3 37.1 %all_to_all.26 = bf16[2,1,128,1024]{3,0,1,2:T(2,128)(2,1)S(1)} all-to-all(bf16[2,1,128,1024]{3,0,1,2:T(2,128)(2,1)S(1)} %copy.17), channel_id=1, replica_groups=mesh['expert'=128,'hidden'=4] {'expert'}, dimensions={2} | all-to-all | bytes 1048576 | tf_op jit(solution)/shard_map/all_to_all | solution.py:20
  48.4 0.9 copy.18
  49.3 0.0 all-gather.3.cloned.1.call-update
  49.3 0.0 copy-done.4
  49.4 39.7 %all-gather.3.cloned.1.call-done = bf16[2,1,512,1024]{3,2,1,0:T(8,128)(2,1)} async-done(((bf16[2,1,128,1024]{3,2,1,0:T(8,128)(2,1)}), bf16[2,1,512,1024]{3,2,1,0:T(8,128)(2,1)}) %all-gather.3.cloned.1.call-update) | async-done | bytes 2097168 | tf_op jit(solution)/shard_map/all_gather | solution.py:21
  89.1 2.7 %fusion.7 = f32[512,1,768]{2,0,1:T(8,128)S(1)} fusion(bf16[1,1024,768]{2,1,0:T(8,128)(2,1)} %param.8, bf16[2,1,512,1024]{3,2,1,0:T(8,128)(2,1)} %all-gather.3.cloned.1.call-done, f32[768]{0:T(1024)S(1)} %reduce.14), kind=kOutput, calls=%fused_computation.11 | convolution fusion | flops 805699584 | bytes 4197376 | tf_op jit(solution)/shard_map/red,edf->ref/dot_general | solution.py:32
  91.8 1.1 copy-done.5
  92.9 1.1 fusion.22
  94.1 6.1 %fusion.19 = bf16[512,1024]{1,0:T(8,128)(2,1)} fusion(bf16[1,1024,768]{2,1,0:T(8,128)(2,1)} %param.8, f32[512,1,768]{2,0,1:T(8,128)} %copy-done.5, bf16[1,768,1024]{2,1,0:T(8,128)(2,1)S(1)} %copy-done, bf16[2,1,512,1024]{3,2,1,0:T(8,128)(2,1)} %all-gather.3.cloned.1.call-done), kind=kOutput, calls=%fused_computation.26 | convolution fusion | flops 1619001344 | bytes 6815744 | tf_op jit(solution)/shard_map/ref,edf->red/dot_general | solution.py:41
  100.1 1.4 maximum_bitcast_fusion
  101.5 45.0 %all_to_all.27 = bf16[4,2,128,1,1024]{4,2,3,1,0:T(8,128)(2,1)} all-to-all(bf16[4,2,128,1,1024]{4,2,3,1,0:T(8,128)(2,1)S(1)} %maximum_bitcast_fusion), channel_id=1, replica_groups=mesh['expert'=128,'hidden'=4] {'hidden'}, dimensions={0} | all-to-all | bytes 4194304 | tf_op jit(solution)/shard_map/all_to_all | solution.py:15
  146.6 2.0 %reduce_sum.52 = bf16[2,128,1024]{2,1,0:T(8,128)(2,1)S(1)} reduce(bf16[4,2,128,1,1024]{4,2,3,1,0:T(8,128)(2,1)} %all_to_all.27, bf16[]{:T(256)} %constant.19.clone.1), dimensions={0,3}, to_apply=%region_4.0 | reduce | flops 786432 | bytes 2621442 | tf_op jit(solution)/shard_map/reduce_sum | solution.py:16
  148.6 0.5 copy.21
  149.1 0.0 copy-start.1
  149.2 40.0 %all_to_all.28 = bf16[2,128,1,1024]{3,0,2,1:T(2,128)(2,1)S(1)} all-to-all(bf16[2,128,1,1024]{3,0,2,1:T(2,128)(2,1)S(1)} %copy.21), channel_id=1, replica_groups=mesh['expert'=128,'hidden'=4] {'expert'}, dimensions={1} | all-to-all | bytes 1048576 | tf_op jit(solution)/shard_map/all_to_all | solution.py:26
  189.2 0.7 fusion.83
  189.9 0.3 convolution_bitcast_fusion
  190.2 0.0 copy-start.2
  190.2 0.3 fusion.55
  190.5 1.1 fusion.34
  191.6 0.4 multiply_reduce_fusion.1
  192.0 1.1 fusion.33
  (6 shorter events, 0.0 us)
Async XLA Ops:
  7.2 85.8 %copy-start = (bf16[1,768,1024]{2,1,0:T(8,128)(2,1)S(1)}, bf16[1,768,1024]{2,1,0:T(8,128)(2,1)}, u32[]{:S(2)}) copy-start(bf16[1,768,1024]{2,1,0:T(8,128)(2,1)} %param.10) | copy-start | bytes 4718596
  7.2 3.1 %copy-start.3 = (bf16[1,196,1024]{2,1,0:T(8,128)(2,1)S(1)}, bf16[1,196,1024]{2,1,0:T(8,128)(2,1)}, u32[]{:S(2)}) copy-start(bf16[1,196,1024]{2,1,0:T(8,128)(2,1)} %param.11) | copy-start | bytes 1204228
  7.2 81.9 %all-gather.3.cloned.1.call-start = ((), (), s32[]{:S(2)}) async-start(), calls=%async_computation.3 | async-start | bytes 2621440 | tf_op jit(solution)/shard_map/all_gather | solution.py:21
  11.3 38.1 %copy-start.4 = (f32[1,768]{1,0:T(1,128)S(1)}, f32[1,768]{1,0:T(1,128)}, u32[]{:S(2)}) copy-start(f32[1,768]{1,0:T(1,128)} %param.9) | copy-start | bytes 9220
  91.8 1.2 copy-start.5
  149.1 40.8 %copy-start.1 = (bf16[1,196,1024]{2,1,0:T(8,128)(2,1)S(1)}, bf16[1,196,1024]{2,1,0:T(8,128)(2,1)}, u32[]{:S(2)}) copy-start(bf16[1,196,1024]{2,1,0:T(8,128)(2,1)} %param.6) | copy-start | bytes 1204228
  190.2 1.8 copy-start.2
Sparse Core Ops, SparseCore 0:
  49.5 39.5 all-gather.2
where the time goes:
time: 200 us
  blocking collectives  122 us (61%)
  waiting for transfers between devices  39.7 us (20%)
  matrix products  16.2 us (8%)
  between operations  14.2 us (7%)
  local copies, waits for them, and re-layouts  3.9 us (2%)
  other arithmetic  3.7 us (2%)
    all_to_all x1, blocking collectives, sum_at_owner(): parts = lax.all_to_all(split_up(x, dim, devices), axis, 0, 0, tiled=True)  45 us
    all_to_all x1, blocking collectives, inbound(): lax.all_to_all(summed.astype(jnp.bfloat16), 'expert', split_axis=1, conca...  40 us
    all_gather x1, waiting for transfers between devices, outbound(): return lax.all_gather(moved, 'hidden', axis=1, tiled=True)  39.7 us
    all_to_all x1, blocking collectives, outbound(): lax.all_to_all(stacked, 'expert', split_axis=2, concat_axis=1, tiled=True)  37.1 us
    dot_general x1, matrix products, expert_backward(): jnp.einsum('ref,edf->red', pre_grad, w_in, preferred_element_type=jnp.flo...  6.06 us
  transfers between devices with their start and end apart: 1, of which 1 were waited for; matrix products, arithmetic and copies ran while one was open for 0% of the time, Pallas kernels for 0%

commit v1 on v0

--- a/solution.py
+++ b/solution.py
@@ -2,6 +2,12 @@
 import jax.numpy as jnp
 from jax import lax
 from jax.sharding import PartitionSpec as P
+
+
+def gather_blocks(block, mesh_axis, dim):
+    shards = lax.all_gather(block, mesh_axis, axis=0, tiled=False)
+    whole = jnp.concatenate(shards, axis=dim)
+    return whole
 
 
 def split_up(x, dim, devices):
@@ -18,7 +24,7 @@
 
 def outbound(stacked):
     moved = lax.all_to_all(stacked, "expert", split_axis=2, concat_axis=1, tiled=True)
-    return lax.all_gather(moved, "hidden", axis=1, tiled=True)
+    return gather_blocks(moved, "hidden", 1)
 
 
 def inbound(terms):

time: 200 us -> 201 us (level)
  no operation moved by 1% of the time
where the time goes in v1:
time: 201 us; the launch traced here: 200 us
  blocking collectives  122 us (61%)
  waiting for transfers between devices  39.7 us (20%)
  matrix products  15.2 us (8%)
  between operations  14.2 us (7%)
  local copies, waits for them, and re-layouts  4.8 us (2%)
  other arithmetic  4.02 us (2%)
    all_to_all x1, blocking collectives, sum_at_owner(): parts = lax.all_to_all(split_up(x, dim, devices), axis, 0, 0, tiled=True)  45 us
    all_to_all x1, blocking collectives, inbound(): lax.all_to_all(summed.astype(jnp.bfloat16), 'expert', split_axis=1, conca...  40 us
    all_gather x1, waiting for transfers between devices, gather_blocks(): shards = lax.all_gather(block, mesh_axis, axis=0, tiled=False)  39.7 us
    all_to_all x1, blocking collectives, outbound(): lax.all_to_all(stacked, 'expert', split_axis=2, concat_axis=1, tiled=True)  37.1 us
    dot_general x1, matrix products, expert_backward(): jnp.einsum('ref,edf->red', pre_grad, w_in, preferred_element_type=jnp.flo...  5.78 us
  transfers between devices with their start and end apart: 1, of which 1 were waited for; matrix products, arithmetic and copies ran while one was open for 0% of the time, Pallas kernels for 0%

profile of v1, /device:TPU:1, one launch (start us, length us, event | category | flops | bytes accessed | tf_op | source)
XLA Modules:
  0.0 200.2 jit_solution(16117053878484089036)
XLA Ops:
  7.2 0.0 copy-start
  7.2 0.0 all-gather.3.cloned.1.call-start
  7.2 1.6 fusion.82
  8.8 0.2 fusion.59
  9.0 1.3 fusion.35
  10.3 0.0 copy-done.3
  10.3 0.4 fusion.36
  10.7 0.1 pad_maximum_fusion
  10.7 0.5 copy.18
  11.3 0.0 copy-start.4
  11.3 37.1 %all_to_all.23 = bf16[2,1,128,1024]{3,0,1,2:T(2,128)(2,1)S(1)} all-to-all(bf16[2,1,128,1024]{3,0,1,2:T(2,128)(2,1)S(1)} %copy.18), channel_id=1, replica_groups=mesh['expert'=128,'hidden'=4] {'expert'}, dimensions={2} | all-to-all | bytes 1048576 | tf_op jit(solution)/shard_map/all_to_all | solution.py:26
  48.4 0.9 copy.19
  49.3 0.0 all-gather.3.cloned.1.call-update
  49.4 39.7 %all-gather.3.cloned.1.call-done = bf16[8,1,128,1024]{3,2,1,0:T(8,128)(2,1)} async-done(((bf16[2,1,128,1024]{3,2,1,0:T(8,128)(2,1)}), bf16[8,1,128,1024]{3,2,1,0:T(8,128)(2,1)}) %all-gather.3.cloned.1.call-update) | async-done | bytes 2097168 | tf_op jit(solution)/shard_map/all_gather | solution.py:8
  89.1 1.8 fusion.83
  90.9 0.2 copy-done.5
  91.1 1.0 fusion.7
  92.1 2.1 %fusion.22 = bf16[512,1024]{1,0:T(8,128)(2,1)} fusion(bf16[1,768,1024]{2,1,0:T(8,128)(2,1)S(1)} %copy-done, f32[512,1,768]{2,0,1:T(8,128)S(1)} %fusion.7), kind=kOutput, calls=%fused_computation.27 | convolution fusion | flops 809369600 | bytes 4194304 | tf_op jit(solution)/shard_map/ref,efd->red/dot_general | solution.py:40
  94.2 5.8 %fusion.19 = bf16[512,1024]{1,0:T(8,128)(2,1)} fusion(bf16[1,1024,768]{2,1,0:T(8,128)(2,1)} %param.8, f32[512,1,768]{2,0,1:T(8,128)} %copy-done.6, bf16[512,1024]{1,0:T(8,128)(2,1)S(1)} %bitcast.128, bf16[1,768,1024]{2,1,0:T(8,128)(2,1)S(1)} %copy-done), kind=kOutput, calls=%fused_computation.26 | convolution fusion | flops 1619001344 | bytes 6815744 | tf_op jit(solution)/shard_map/ref,edf->red/dot_general | solution.py:47
  100.0 1.7 maximum_bitcast_fusion
  101.8 45.0 %all_to_all.24 = bf16[4,2,128,1,1024]{4,2,3,1,0:T(8,128)(2,1)} all-to-all(bf16[4,2,128,1,1024]{4,2,3,1,0:T(8,128)(2,1)S(1)} %maximum_bitcast_fusion), channel_id=1, replica_groups=mesh['expert'=128,'hidden'=4] {'hidden'}, dimensions={0} | all-to-all | bytes 4194304 | tf_op jit(solution)/shard_map/all_to_all | solution.py:21
  146.8 2.0 %reduce_sum.52 = bf16[2,128,1024]{2,1,0:T(8,128)(2,1)S(1)} reduce(bf16[4,2,128,1,1024]{4,2,3,1,0:T(8,128)(2,1)} %all_to_all.24, bf16[]{:T(256)} %constant.19.clone.1), dimensions={0,3}, to_apply=%region_4.0 | reduce | flops 786432 | bytes 2621442 | tf_op jit(solution)/shard_map/reduce_sum | solution.py:22
  148.8 0.5 copy.22
  149.4 0.0 copy-start.1
  149.4 40.0 %all_to_all.25 = bf16[2,128,1,1024]{3,0,2,1:T(2,128)(2,1)S(1)} all-to-all(bf16[2,128,1,1024]{3,0,2,1:T(2,128)(2,1)S(1)} %copy.22), channel_id=1, replica_groups=mesh['expert'=128,'hidden'=4] {'expert'}, dimensions={1} | all-to-all | bytes 1048576 | tf_op jit(solution)/shard_map/all_to_all | solution.py:32
  189.4 0.7 fusion.84
  190.2 0.3 convolution_bitcast_fusion
  190.4 0.0 copy-start.2
  190.5 0.3 fusion.55
  190.7 1.1 fusion.34
  191.8 0.4 multiply_reduce_fusion.1
  192.2 1.1 fusion.33
  (9 shorter events, 0.0 us)
Async XLA Ops:
  7.2 84.9 %copy-start = (bf16[1,768,1024]{2,1,0:T(8,128)(2,1)S(1)}, bf16[1,768,1024]{2,1,0:T(8,128)(2,1)}, u32[]{:S(2)}) copy-start(bf16[1,768,1024]{2,1,0:T(8,128)(2,1)} %param.10) | copy-start | bytes 4718596
  7.2 3.1 %copy-start.3 = (bf16[1,196,1024]{2,1,0:T(8,128)(2,1)S(1)}, bf16[1,196,1024]{2,1,0:T(8,128)(2,1)}, u32[]{:S(2)}) copy-start(bf16[1,196,1024]{2,1,0:T(8,128)(2,1)} %param.11) | copy-start | bytes 1204228
  7.2 81.9 %all-gather.3.cloned.1.call-start = ((), (), s32[]{:S(2)}) async-start(), calls=%async_computation.3 | async-start | bytes 2621440 | tf_op jit(solution)/shard_map/all_gather | solution.py:8
  11.3 38.1 %copy-start.4 = (f32[1,768]{1,0:T(1,128)S(1)}, f32[1,768]{1,0:T(1,128)}, u32[]{:S(2)}) copy-start(f32[1,768]{1,0:T(1,128)} %param.9) | copy-start | bytes 9220
  89.1 2.0 %copy-start.5 = (bf16[1,1024,768]{2,1,0:T(8,128)(2,1)S(1)}, bf16[1,1024,768]{2,1,0:T(8,128)(2,1)}, u32[]{:S(2)}) copy-start(bf16[1,1024,768]{2,1,0:T(8,128)(2,1)} %param.8) | copy-start | bytes 4718596
  92.1 2.1 %copy-start.6 = (f32[512,1,768]{2,0,1:T(8,128)}, f32[512,1,768]{2,0,1:T(8,128)S(1)}, u32[]{:S(2)}) copy-start(f32[512,1,768]{2,0,1:T(8,128)S(1)} %fusion.7) | copy-start | bytes 4718596
  149.4 40.8 %copy-start.1 = (bf16[1,196,1024]{2,1,0:T(8,128)(2,1)S(1)}, bf16[1,196,1024]{2,1,0:T(8,128)(2,1)}, u32[]{:S(2)}) copy-start(bf16[1,196,1024]{2,1,0:T(8,128)(2,1)} %param.6) | copy-start | bytes 1204228
  190.4 1.8 copy-start.2
Sparse Core Ops, SparseCore 0:
  49.5 39.5 all-gather.2
